TPU v7x, 32 devices: a whole 2x2x4 slice. The times are simulated.
32 devices in a mesh: grp: 4 (over y, x), dom: 8 (over z, core).
Axes of the slice: x: 2, y: 2, z: 4, core: 2. Of those that a mesh axis runs over, the one named last changes fastest.
Arguments:
- fields: float32 [210, 32768], P(None, ('grp', 'dom')), may hold values from -6 to 6
- metric: float32 [9, 32768], P(None, ('grp', 'dom')), may hold values from -5 to 5
- normals: float32 [12, 32768], P(None, ('grp', 'dom')), may hold values from -3 to 3
- fscale: float32 [4, 32768], P(None, ('grp', 'dom')), may hold values from 0.5 to 4
- orders: int32 [32768], P(('grp', 'dom')), may hold values from 1 to 4, as said below
- slots: int32 [32768], P(('grp', 'dom')), may hold values from 0 to 511, as said below
- send_faces: int32 [294912], P(('grp', 'dom')), may hold values from 0 to 8192, as said below
- recv_faces: int32 [262144], P(('grp', 'dom')), may hold values from 0 to 9216, as said below
- dmat: float32 [4, 105, 35], P('grp'), may hold values from -4 to 4
- tmat: float32 [4, 60, 35], P('grp'), may hold values from -4 to 4
- lmat: float32 [4, 35, 60], P('grp'), may hold values from -3 to 3
Outputs:
- rhs: float32 [210, 65536], P(None, ('grp', 'dom'))
Inputs may be any that keep to these rules, and one draw needn't show every extreme that they name: `orders`: on each device every order from 1 to 4 is held by at least one element and by at most 512; one order is held by exactly 512. The elements of one device that share an order have distinct slots. `send_faces`: each entry names a face of an occupied slot of the sending bucket or equals 4 * 2048 (nothing); in each list the items in use stand first. `recv_faces`: every face of an occupied slot names a distinct received item that is in use, and every item in use is named by exactly one face; faces of empty slots hold 9216. A list carries at most 768 items in use, and some list carries exactly 768.
All inputs are finite; a program needn't handle non-finite values.
Results may differ from a plain program's by a relative error of at most 0.0003.
Values sent between devices are 32-bit elements; how exact they have to be, the bound alone decides.
A program may use at most 128 MiB of HBM per device.

v0:
```python
import jax
import jax.numpy as jnp
from jax import lax
from jax.sharding import PartitionSpec as P

NPM = 35
FPTS = 15
exact_prec = lax.Precision.HIGHEST


def shifted(x, axis, by):
    size = lax.axis_size(axis)
    return lax.ppermute(x, axis, [(i, (i + by) % size) for i in range(size)])


def order_mask(order_index):
    node_total = (order_index + 2) * (order_index + 3) * (order_index + 4) // 6
    return (jnp.arange(NPM, dtype=jnp.int32) < node_total).astype(jnp.float32)


def cross_of(first_vec, second_vec):
    return [
        first_vec[1] * second_vec[2] - first_vec[2] * second_vec[1],
        first_vec[2] * second_vec[0] - first_vec[0] * second_vec[2],
        first_vec[0] * second_vec[1] - first_vec[1] * second_vec[0],
    ]


def volume_terms(coefficients, metric_cols, deriv_mats):
    derived = jnp.einsum("anm,qms->qans", deriv_mats, coefficients, precision=exact_prec)

    def partial_of(component, direction):
        return (
            metric_cols[0, direction][None] * derived[component, 0]
            + metric_cols[1, direction][None] * derived[component, 1]
            + metric_cols[2, direction][None] * derived[component, 2]
        )

    curl_h = [
        partial_of(5, 1) - partial_of(4, 2),
        partial_of(3, 2) - partial_of(5, 0),
        partial_of(4, 0) - partial_of(3, 1),
    ]
    curl_e = [
        partial_of(2, 1) - partial_of(1, 2),
        partial_of(0, 2) - partial_of(2, 0),
        partial_of(1, 0) - partial_of(0, 1),
    ]
    return jnp.stack(curl_h + [-value for value in curl_e], 0)


def face_flux(own_traces, neighbour, normal_cols, scale_cols):
    own_split = own_traces.reshape(6, FPTS, -1)
    far_split = neighbour.reshape(6, FPTS, -1)
    jump_e = [far_split[c] - own_split[c] for c in range(3)]
    jump_h = [far_split[c + 3] - own_split[c + 3] for c in range(3)]
    normal = [normal_cols[c] for c in range(3)]
    normal_e = normal[0] * jump_e[0] + normal[1] * jump_e[1] + normal[2] * jump_e[2]
    normal_h = normal[0] * jump_h[0] + normal[1] * jump_h[1] + normal[2] * jump_h[2]
    turn_h = cross_of(normal, jump_h)
    turn_e = cross_of(normal, jump_e)
    flux_e = [0.5 * scale_cols * (turn_h[c] + jump_e[c] - normal[c] * normal_e) for c in range(3)]
    flux_h = [0.5 * scale_cols * (-turn_e[c] + jump_h[c] - normal[c] * normal_h) for c in range(3)]
    return jnp.stack(flux_e + flux_h, 0)


def block_rhs(bucket, own_traces, neighbour, deriv_mats, lift_mat):
    slot_count = bucket.shape[1]
    coefficients = bucket[: 6 * NPM].reshape(6, NPM, slot_count)
    metric_cols = bucket[6 * NPM : 6 * NPM + 9].reshape(3, 3, slot_count)
    normal_cols = bucket[6 * NPM + 9 : 6 * NPM + 21].reshape(3, 1, 4 * slot_count)
    scale_cols = bucket[6 * NPM + 21 : 6 * NPM + 25].reshape(1, 4 * slot_count)
    volume = volume_terms(coefficients, metric_cols, deriv_mats)
    flux = face_flux(own_traces, neighbour, normal_cols, scale_cols).reshape(
        6, FPTS * 4, slot_count
    )
    lifted = jnp.einsum("mp,qps->qms", lift_mat, flux, precision=exact_prec)
    return (volume + lifted).reshape(6 * NPM, slot_count)


def across_groups(outgoing):
    return lax.all_to_all(outgoing, "grp", split_axis=1, concat_axis=1, tiled=True)


def across_columns(outgoing):
    lowered = shifted(outgoing[0], "dom", -1)
    raised = shifted(outgoing[2], "dom", 1)
    return jnp.stack([lowered, outgoing[1], raised], 0)


def local(fields, metric, normals, fscale, orders, slots, send_faces, recv_faces, dmat, tmat, lmat):
    own_group = lax.axis_index("grp")
    groups = lax.axis_size("grp")
    elements = fields.shape[1]
    capacity = elements // 2
    slot_count = groups * capacity
    payload = jnp.concatenate([fields, metric, normals, fscale], 0)
    row_count = payload.shape[0]
    zero_column = jnp.zeros((row_count, 1), jnp.float32)
    target = (orders - 1) * capacity + slots
    inverse = (
        jnp.full((slot_count,), elements, jnp.int32)
        .at[target]
        .set(jnp.arange(elements, dtype=jnp.int32))
    )
    padded = jnp.concatenate([payload, zero_column], 1)
    outgoing = jnp.take(padded, inverse, axis=1).reshape(row_count, groups, capacity)
    bucket = lax.all_to_all(outgoing, "grp", split_axis=1, concat_axis=1, tiled=True).reshape(
        row_count, slot_count
    )
    node_mask = order_mask(own_group)
    deriv_mats = dmat[0].reshape(3, NPM, NPM) * node_mask[None, :, None] * node_mask[None, None, :]
    trace_mat = tmat[0] * node_mask[None, :]
    lift_mat = lmat[0] * node_mask[:, None]
    coefficients = bucket[: 6 * NPM].reshape(6, NPM, slot_count)
    own_traces = jnp.einsum("pm,qms->qps", trace_mat, coefficients, precision=exact_prec).reshape(
        6 * FPTS, 4 * slot_count
    )
    face_rows = jnp.concatenate([own_traces.T, jnp.zeros((1, 6 * FPTS), jnp.float32)], 0)
    list_total = send_faces.shape[0]
    list_size = list_total // (3 * groups)
    outgoing_faces = jnp.take(face_rows, send_faces, axis=0).reshape(3, groups, list_size, 6 * FPTS)
    arrived = across_columns(across_groups(outgoing_faces))
    received = jnp.concatenate(
        [arrived.reshape(list_total, 6 * FPTS), jnp.zeros((1, 6 * FPTS), jnp.float32)], 0
    )
    neighbour = jnp.take(received, recv_faces, axis=0).T
    return block_rhs(bucket, own_traces, neighbour, deriv_mats, lift_mat)


def solution(mesh):
    in_specs = (
        P(None, ("grp", "dom")),
        P(None, ("grp", "dom")),
        P(None, ("grp", "dom")),
        P(None, ("grp", "dom")),
        P(("grp", "dom")),
        P(("grp", "dom")),
        P(("grp", "dom")),
        P(("grp", "dom")),
        P("grp", None, None),
        P("grp", None, None),
        P("grp", None, None),
    )
    out_specs = P(None, ("grp", "dom"))
    return jax.shard_map(local, mesh=mesh, in_specs=in_specs, out_specs=out_specs, check_vma=False)
```

profile of v0, /device:TPU:1, one launch (start us, length us, event | category | flops | bytes accessed | tf_op | source)
XLA Modules:
  0.0 281.7 jit_solution(4036362159378918942)
XLA Ops:
  0.7 4.3 %scatter_custom_fusion = s32[2048]{0:T(1024)S(1)} fusion(s32[1024]{0:T(1024)S(1)} %compare_select_fusion.3, s32[1024]{0:T(1024)S(1)} %iota.14, s32[]{:T(128)} %constant.33.clone.1), kind=kCustom, calls=%fused_computation.79 | custom fusion | bytes 8196 | tf_op jit(solution)/shard_map/scatter | solution.py:104
  11.3 6.6 %gather_fusion = f32[2048,235]{1,0:T(8,128)S(1)} fusion(f32[235,1025]{0,1:T(8,128)S(1)} %select_maximum_fusion, s32[2048]{0:T(1024)S(1)} %fusion.11), kind=kCustom, calls=%fused_computation | custom fusion | bytes 3858432 | tf_op jit(solution)/shard_map/jit(_take)/gather | solution.py:107
  19.8 3.1 %broadcast_select_fusion.1 = f32[235,4,512]{2,0,1:T(8,128)} fusion(f32[235,4,512]{2,0,1:T(8,128)} %copy.62, pred[4,512]{1,0:T(4,128)(4,1)S(1)} %broadcast_in_dim.53), kind=kLoop, calls=%fused_computation.20 | loop fusion | flops 481280 | bytes 3852288 | tf_op jit(solution)/shard_map/jit(_take)/select_n | solution.py:107
  22.9 4.4 %all-to-all-start = ((f32[235,4,512]{2,0,1:T(8,128)}), f32[235,4,512]{2,0,1:T(8,128)S(1)}, u32[]{:S(2)}, u32[]{:S(2)}) async-start(f32[235,4,512]{2,0,1:T(8,128)} %broadcast_select_fusion.1), calls=%async_computation | async-start | bytes 3932160 | tf_op jit(solution)/shard_map/all_to_all | solution.py:108
  29.8 20.6 %all-to-all-done = f32[235,4,512]{2,0,1:T(8,128)S(1)} async-done(((f32[235,4,512]{2,0,1:T(8,128)}), f32[235,4,512]{2,0,1:T(8,128)S(1)}, u32[]{:S(2)}, u32[]{:S(2)}) %all-to-all-start) | async-done | bytes 1925152 | tf_op jit(solution)/shard_map/all_to_all | solution.py:108
  58.0 4.7 %convolution_bitcast_fusion.1 = f32[6,60,2048]{2,1,0:T(8,128)S(1)} fusion(f32[6,35,2048]{2,1,0:T(8,128)} %reshape.2020, f32[1,60,35]{1,0,2:T(1,128)S(1)} %broadcast_multiply_fusion), kind=kOutput, calls=%fused_computation.7 | convolution fusion | flops 309657600 | bytes 4677840 | tf_op jit(solution)/shard_map/pm,qms->qps/dot_general | solution.py:116
  62.7 3.0 %reshape.2021 = f32[90,8192]{1,0:T(8,128)} reshape(f32[6,60,2048]{2,1,0:T(8,128)S(1)} %convolution_bitcast_fusion.1) | data formatting | bytes 5898240 | tf_op jit(solution)/shard_map/reshape | solution.py:116
  65.7 5.2 %copy.67 = f32[90,8192]{0,1:T(8,128)} copy(f32[90,8192]{1,0:T(8,128)} %reshape.2021) | data formatting | bytes 5898240 | tf_op jit(solution)/shard_map/reshape | solution.py:116
  70.8 3.8 %concatenate.15 = f32[8193,90]{1,0:T(8,128)} pad(f32[8192,90]{1,0:T(8,128)} %bitcast.170, f32[]{:T(128)} %constant.45.clone.1), padding=0_1x0_0 | pad | bytes 5898604 | tf_op jit(solution)/shard_map/concatenate | solution.py:119
  74.6 33.3 %gather_fusion.1 = f32[9216,90]{1,0:T(8,128)} fusion(f32[8193,90]{1,0:T(8,128)} %concatenate.15, s32[9216]{0:T(1024)S(1)} %fusion.3), kind=kCustom, calls=%fused_computation.1 | custom fusion | bytes 6672384 | tf_op jit(solution)/shard_map/jit(_take)/gather | solution.py:122
  107.9 3.9 %copy.68 = f32[3,4,768,90]{2,3,0,1:T(8,128)S(1)} copy(f32[3,4,768,90]{3,2,1,0:T(8,128)} %bitcast.168) | data formatting | bytes 6635520 | tf_op jit(solution)/shard_map/jit(_take)/gather | solution.py:122
  114.1 4.0 %all-to-all-start.1 = ((f32[3,4,768,90]{2,3,0,1:T(8,128)}), f32[3,4,768,90]{2,3,0,1:T(8,128)S(1)}, u32[]{:S(2)}, u32[]{:S(2)}) async-start(f32[3,4,768,90]{2,3,0,1:T(8,128)} %broadcast_select_fusion), calls=%async_computation.1 | async-start | bytes 7077888 | tf_op jit(solution)/shard_map/all_to_all | solution.py:82
  118.0 10.5 %convolution_bitcast_fusion = f32[6,3,35,2048]{3,2,1,0:T(8,128)} fusion(f32[6,35,2048,1]{2,1,0,3:T(8,128)} %reshape.2060, f32[3,35,35]{2,1,0:T(8,128)} %copy.65), kind=kOutput, calls=%fused_computation.5 | convolution fusion | flops 541900800 | bytes 6895980 | tf_op jit(solution)/shard_map/anm,qms->qans/dot_general | solution.py:30
  142.4 15.2 %all-to-all-done.1 = f32[3,4,768,90]{2,3,0,1:T(8,128)S(1)} async-done(((f32[3,4,768,90]{2,3,0,1:T(8,128)}), f32[3,4,768,90]{2,3,0,1:T(8,128)S(1)}, u32[]{:S(2)}, u32[]{:S(2)}) %all-to-all-start.1) | async-done | bytes 3317792 | tf_op jit(solution)/shard_map/all_to_all | solution.py:82
  174.3 7.7 %collective-permute-done.1 = f32[4,768,90]{1,0,2:T(4,128)S(1)} collective-permute-done((f32[4,768,90]{1,0,2:T(4,128)S(1)}, f32[4,768,90]{1,0,2:T(4,128)S(1)}, u32[]{:S(2)}, u32[]{:S(2)}) %collective-permute-start.1) | collective-permute-done | bytes 1105952 | tf_op jit(solution)/shard_map/ppermute | solution.py:13
  182.3 6.7 %collective-permute-done = f32[4,768,90]{1,0,2:T(4,128)} collective-permute-done((f32[4,768,90]{1,0,2:T(4,128)}, f32[4,768,90]{1,0,2:T(4,128)}, u32[]{:S(2)}, u32[]{:S(2)}) %collective-permute-start) | collective-permute-done | bytes 1105952 | tf_op jit(solution)/shard_map/ppermute | solution.py:13
  190.7 3.6 %copy.73 = f32[3,4,768,90]{3,2,1,0:T(8,128)} copy(f32[3,4,768,90]{2,3,0,1:T(8,128)S(1)} %pad_maximum_fusion) | data formatting | bytes 6635520 | tf_op jit(solution)/shard_map/stack | solution.py:88
  194.3 4.0 %concatenate.16 = f32[9217,90]{1,0:T(8,128)} pad(f32[9216,90]{1,0:T(8,128)} %bitcast.169, f32[]{:T(128)} %constant.45.clone.1), padding=0_1x0_0 | pad | bytes 6635884 | tf_op jit(solution)/shard_map/concatenate | solution.py:124
  198.3 30.1 %gather_fusion.2 = f32[8192,90]{1,0:T(8,128)} fusion(f32[9217,90]{1,0:T(8,128)} %concatenate.16, s32[8192]{0:T(1024)S(1)} %copy-done.25), kind=kCustom, calls=%fused_computation.2 | custom fusion | bytes 5931008 | tf_op jit(solution)/shard_map/jit(_take)/gather | solution.py:127
  228.4 6.2 %select_bitcast_fusion = f32[90,8192]{0,1:T(8,128)S(1)} fusion(f32[8192,90]{1,0:T(8,128)} %gather_fusion.2, pred[8192]{0:T(1024)(128)(4,1)S(1)} %copy-done.26), kind=kLoop, calls=%fused_computation.4 | loop fusion | flops 737280 | bytes 5906432 | tf_op jit(solution)/shard_map/jit(_take)/select_n | solution.py:127
  234.6 11.1 %fusion.14 = (f32[15,8192]{0,1:T(8,128)}, f32[15,8192]{0,1:T(8,128)}, f32[15,8192]{0,1:T(8,128)}, f32[15,8192]{0,1:T(8,128)}, f32[15,8192]{0,1:T(8,128)}, /*index=5*/f32[15,8192]{0,1:T(8,128)}) fusion(f32[90,8192]{0,1:T(8,128)S(1)} %select_bitcast_fusion), kind=kLoop, calls=%fused_computation.82 | loop fusion | bytes 5898240 | tf_op jit(solution)/shard_map/slice | solution.py:56
  264.7 3.7 %copy.79 = f32[15,8192]{1,0:T(8,128)} copy(f32[15,8192]{0,1:T(8,128)} %get-tuple-element.13) | data formatting | bytes 983040 | tf_op jit(solution)/shard_map/slice | solution.py:56
  270.4 3.2 %multiply_dynamic-update-slice_fusion.5 = (f32[6,60,2048]{2,1,0:T(8,128)S(1)}, f32[1,60,2048]{2,1,0:T(8,128)S(1)}, f32[1,60,2048]{2,1,0:T(8,128)S(1)}, f32[1,60,...) fusion(f32[1,60,2048]{2,1,0:T(8,128)} %mul.929, f32[1,60,2048]{2,1,0:T(8,128)} %mul.943, ...), kind=kLoop, calls=%fused_computation.33 | loop fusion | flops 2088959 | bytes 10027008
  276.1 4.2 %fusion = f32[6,35,2048]{2,1,0:T(8,128)S(1)} fusion(f32[6,35,2048]{2,1,0:T(8,128)} %negate_dynamic-update-slice_fusion, f32[6,60,2048]{2,1,0:T(8,128)S(1)} %multiply_dynamic-update-slice_fusion, f32[1,35,60]{2,0,1:T(1,128)S(1)} %copy-done.27, f32[35]{0:T(128)S(1)} %copy-done.32), kind=kOutput, calls=%fused_computation.9 | convolution fusion | flops 310089792 | bytes 6398300 | tf_op jit(solution)/shard_map/mp,qps->qms/dot_general | solution.py:77
  (139 shorter events, 78.2 us)
Async XLA Ops:
  0.0 8.7 %copy-start.30 = (f32[4,1024]{1,0:T(4,128)S(1)}, f32[4,1024]{1,0:T(4,128)}, u32[]{:S(2)}) copy-start(f32[4,1024]{1,0:T(4,128)} %param.14) | copy-start | bytes 49156
  19.7 7.6 %copy-start.23 = (s32[9216]{0:T(1024)S(1)}, s32[9216]{0:T(1024)}, u32[]{:S(2)}) copy-start(s32[9216]{0:T(1024)} %param.17) | copy-start | bytes 110596
  19.7 7.8 %copy-start.28 = (f32[1,105,35]{1,0,2:T(1,128)S(1)}, f32[1,105,35]{1,0,2:T(1,128)}, u32[]{:S(2)}) copy-start(f32[1,105,35]{1,0,2:T(1,128)} %param.19) | copy-start | bytes 44104
  19.8 8.7 %copy-start.29 = (f32[1,60,35]{1,0,2:T(1,128)S(1)}, f32[1,60,35]{1,0,2:T(1,128)}, u32[]{:S(2)}) copy-start(f32[1,60,35]{1,0,2:T(1,128)} %param.20) | copy-start | bytes 25204
  22.9 5.7 %copy-start.24 = (s32[8192]{0:T(1024)S(1)}, s32[8192]{0:T(1024)}, u32[]{:S(2)}) copy-start(s32[8192]{0:T(1024)} %param.18) | copy-start | bytes 98308
  22.9 27.5 %all-to-all-start = ((f32[235,4,512]{2,0,1:T(8,128)}), f32[235,4,512]{2,0,1:T(8,128)S(1)}, u32[]{:S(2)}, u32[]{:S(2)}) async-start(f32[235,4,512]{2,0,1:T(8,128)} %broadcast_select_fusion.1), calls=%async_computation | async-start | bytes 3932160 | tf_op jit(solution)/shard_map/all_to_all | solution.py:108
  27.4 25.5 %copy-start.31 = (f32[35]{0:T(128)}, f32[35]{0:T(128)S(1)}, u32[]{:S(2)}) copy-start(f32[35]{0:T(128)S(1)} %compare_convert_fusion) | copy-start | bytes 424
  114.1 43.5 %all-to-all-start.1 = ((f32[3,4,768,90]{2,3,0,1:T(8,128)}), f32[3,4,768,90]{2,3,0,1:T(8,128)S(1)}, u32[]{:S(2)}, u32[]{:S(2)}) async-start(f32[3,4,768,90]{2,3,0,1:T(8,128)} %broadcast_select_fusion), calls=%async_computation.1 | async-start | bytes 7077888 | tf_op jit(solution)/shard_map/all_to_all | solution.py:82
  132.8 7.2 %copy-start.9 = (f32[1,1,2048]{2,1,0:T(1,128)}, f32[1,1,2048]{2,1,0:T(1,128)S(1)}, u32[]{:S(2)}) copy-start(f32[1,1,2048]{2,1,0:T(1,128)S(1)} %get-tuple-element.28) | copy-start | bytes 24580
  132.8 7.2 %copy-start.11 = (f32[1,1,2048]{2,1,0:T(1,128)}, f32[1,1,2048]{2,1,0:T(1,128)S(1)}, u32[]{:S(2)}) copy-start(f32[1,1,2048]{2,1,0:T(1,128)S(1)} %get-tuple-element.32) | copy-start | bytes 24580
  132.8 7.2 %copy-start.13 = (f32[1,1,2048]{2,1,0:T(1,128)}, f32[1,1,2048]{2,1,0:T(1,128)S(1)}, u32[]{:S(2)}) copy-start(f32[1,1,2048]{2,1,0:T(1,128)S(1)} %get-tuple-element.33) | copy-start | bytes 24580
  132.8 7.2 %copy-start.15 = (f32[1,1,2048]{2,1,0:T(1,128)}, f32[1,1,2048]{2,1,0:T(1,128)S(1)}, u32[]{:S(2)}) copy-start(f32[1,1,2048]{2,1,0:T(1,128)S(1)} %get-tuple-element.34) | copy-start | bytes 24580
  132.8 7.2 %copy-start.17 = (f32[1,1,2048]{2,1,0:T(1,128)}, f32[1,1,2048]{2,1,0:T(1,128)S(1)}, u32[]{:S(2)}) copy-start(f32[1,1,2048]{2,1,0:T(1,128)S(1)} %get-tuple-element.29) | copy-start | bytes 24580
  132.8 7.2 %copy-start.19 = (f32[1,1,2048]{2,1,0:T(1,128)}, f32[1,1,2048]{2,1,0:T(1,128)S(1)}, u32[]{:S(2)}) copy-start(f32[1,1,2048]{2,1,0:T(1,128)S(1)} %get-tuple-element.30) | copy-start | bytes 24580
  132.8 7.2 %copy-start.21 = (f32[1,1,2048]{2,1,0:T(1,128)}, f32[1,1,2048]{2,1,0:T(1,128)S(1)}, u32[]{:S(2)}) copy-start(f32[1,1,2048]{2,1,0:T(1,128)S(1)} %get-tuple-element.31) | copy-start | bytes 24580
  159.5 22.5 %collective-permute-start.1 = (f32[4,768,90]{1,0,2:T(4,128)S(1)}, f32[4,768,90]{1,0,2:T(4,128)S(1)}, u32[]{:S(2)}, u32[]{:S(2)}) collective-permute-start(f32[4,768,90]{1,0,2:T(4,128)S(1)} %copy.71), channel_id=1, source_target_pairs={{0,1},{1,2},{2,3},{3,4},{4,5},{5,6},{6,7},{7,0},{8,9},{9,10},{10,1... | collective-permute-start | bytes 3317768 | tf_op jit(solution)/shard_map/ppermute | solution.py:13
  164.0 25.0 %collective-permute-start = (f32[4,768,90]{1,0,2:T(4,128)}, f32[4,768,90]{1,0,2:T(4,128)}, u32[]{:S(2)}, u32[]{:S(2)}) collective-permute-start(f32[4,768,90]{1,0,2:T(4,128)} %copy.69), channel_id=1, source_target_pairs={{0,7},{1,0},{2,1},{3,2},{4,3},{5,4},{6,5},{7,6},{8,15},{9,8},{10,9... | collective-permute-start | bytes 3317768 | tf_op jit(solution)/shard_map/ppermute | solution.py:13
  165.1 4.4 %copy-start.10 = (f32[1,1,2048]{2,1,0:T(1,128)S(1)}, f32[1,1,2048]{2,1,0:T(1,128)}, u32[]{:S(2)}) copy-start(f32[1,1,2048]{2,1,0:T(1,128)} %copy-done.9) | copy-start | bytes 24580
  166.3 5.6 %copy-start.12 = (f32[1,1,2048]{2,1,0:T(1,128)S(1)}, f32[1,1,2048]{2,1,0:T(1,128)}, u32[]{:S(2)}) copy-start(f32[1,1,2048]{2,1,0:T(1,128)} %copy-done.11) | copy-start | bytes 24580
  166.3 5.6 %copy-start.14 = (f32[1,1,2048]{2,1,0:T(1,128)S(1)}, f32[1,1,2048]{2,1,0:T(1,128)}, u32[]{:S(2)}) copy-start(f32[1,1,2048]{2,1,0:T(1,128)} %copy-done.13) | copy-start | bytes 24580
  166.3 5.6 %copy-start.16 = (f32[1,1,2048]{2,1,0:T(1,128)S(1)}, f32[1,1,2048]{2,1,0:T(1,128)}, u32[]{:S(2)}) copy-start(f32[1,1,2048]{2,1,0:T(1,128)} %copy-done.15) | copy-start | bytes 24580
  171.8 18.6 %copy-start.7 = (f32[1,4,768,90]{2,3,0,1:T(8,128)S(1)}, f32[1,4,768,90]{2,3,0,1:T(8,128)}, u32[]{:S(2)}) copy-start(f32[1,4,768,90]{2,3,0,1:T(8,128)} %get-tuple-element.21) | copy-start | bytes 3317764
  198.3 30.1 %copy-start.26 = (pred[8192]{0:T(1024)(128)(4,1)S(1)}, pred[8192]{0:T(1024)(128)(4,1)}, u32[]{:S(2)}) copy-start(pred[8192]{0:T(1024)(128)(4,1)} %compare_and_fusion.1) | copy-start | bytes 24580
  264.7 5.7 %copy-start.1 = (f32[6,60,2048]{2,1,0:T(8,128)S(1)}, f32[6,60,2048]{2,1,0:T(8,128)}, u32[]{:S(2)}) copy-start(f32[6,60,2048]{2,1,0:T(8,128)} %copy-done) | copy-start | bytes 8847364
  (13 other events, 38.9 us)
where the time goes:
time: 283 us; the launch traced here: 282 us
  local copies, waits for them, and re-layouts  164 us (58%)
  waiting for transfers between devices  50.2 us (18%)
  other arithmetic  36.3 us (13%)
  matrix products  19.4 us (7%)
  starting transfers between devices  11.1 us (4%)
    gather x2, local copies, waits for them, and re-layouts, local(): jnp.take(face_rows, send_faces, axis=0)  37.2 us
    gather x1, local copies, waits for them, and re-layouts, local(): neighbour = jnp.take(received, recv_faces, axis=0).T  30.1 us
    all_to_all x1, waiting for transfers between devices, local(): lax.all_to_all(outgoing, 'grp', split_axis=1, concat_axis=1, tiled=True)  20.6 us
    slice x4, local copies, waits for them, and re-layouts, face_flux(): jump_h = [far_split[c + 3] - own_split[c + 3] for c in range(3)]  20.5 us
    unnamed x10, other arithmetic  16.7 us
    all_to_all x1, waiting for transfers between devices, across_groups(): lax.all_to_all(outgoing, 'grp', split_axis=1, concat_axis=1, tiled=True)  15.2 us
    ppermute x2, waiting for transfers between devices, shifted(): return lax.ppermute(x, axis, [(i, (i + by) % size) for i in range(size)])  14.4 us
    dot_general x1, matrix products, volume_terms(): jnp.einsum('anm,qms->qans', deriv_mats, coefficients, precision=exact_prec)  10.5 us
  transfers between devices with their start and end apart: 4, of which 4 were waited for; matrix products, arithmetic and copies ran while one was open for 14% of the time, Pallas kernels for 0%

commit v1 on v0

--- a/solution.py
+++ b/solution.py
@@ -2,6 +2,7 @@
 import jax.numpy as jnp
 from jax import lax
 from jax.sharding import PartitionSpec as P
+from jax.lax import all_to_all, axis_size
 
 NPM = 35
 FPTS = 15
@@ -105,9 +106,15 @@
     )
     padded = jnp.concatenate([payload, zero_column], 1)
     outgoing = jnp.take(padded, inverse, axis=1).reshape(row_count, groups, capacity)
-    bucket = lax.all_to_all(outgoing, "grp", split_axis=1, concat_axis=1, tiled=True).reshape(
-        row_count, slot_count
-    )
+    bucket = jnp.concatenate(
+        all_to_all(
+            jnp.stack(jnp.split(outgoing, axis_size("grp"), axis=1), axis=0),
+            axis_name="grp",
+            split_axis=0,
+            concat_axis=0,
+        ),
+        1,
+    ).reshape(row_count, slot_count)
     node_mask = order_mask(own_group)
     deriv_mats = dmat[0].reshape(3, NPM, NPM) * node_mask[None, :, None] * node_mask[None, None, :]
     trace_mat = tmat[0] * node_mask[None, :]

time: 283 us -> 290 us (1.025); the launches traced: 282 us -> 285 us
    another operation x0 -> x1, other arithmetic: none -> 3.2 us  [local(): jnp.stack(jnp.split(outgoing, axis_size('grp'), axis=1), axis=0)]
    unnamed x10 -> x11, other arithmetic: 16.7 us -> 17.5 us
    unnamed x70 -> x76, local copies, waits for them, and re-layouts: 6.34 us -> 5.64 us
  transfers between devices with their start and end apart: 4 -> 4, of which waited for: 4 -> 4; matrix products, arithmetic and copies ran while one was open for 14% -> 13% of each run, Pallas kernels for 0% -> 0%
where the time goes in v1:
time: 290 us; the launch traced here: 285 us
  local copies, waits for them, and re-layouts  164 us (57%)
  waiting for transfers between devices  50.1 us (17%)
  other arithmetic  37.9 us (13%)
  matrix products  19.4 us (7%)
  starting transfers between devices  11.9 us (4%)
    gather x2, local copies, waits for them, and re-layouts, local(): jnp.take(face_rows, send_faces, axis=0)  37.2 us
    gather x1, local copies, waits for them, and re-layouts, local(): neighbour = jnp.take(received, recv_faces, axis=0).T  30 us
    slice x4, local copies, waits for them, and re-layouts, face_flux(): jump_h = [far_split[c + 3] - own_split[c + 3] for c in range(3)]  20.7 us
    all_to_all x1, waiting for transfers between devices, local(): all_to_all(jnp.stack(jnp.split(outgoing, axis_size('grp'), axis=1), axis=...  20 us
    unnamed x11, other arithmetic  17.5 us
    all_to_all x1, waiting for transfers between devices, across_groups(): lax.all_to_all(outgoing, 'grp', split_axis=1, concat_axis=1, tiled=True)  15.5 us
    ppermute x2, waiting for transfers between devices, shifted(): return lax.ppermute(x, axis, [(i, (i + by) % size) for i in range(size)])  14.5 us
    dot_general x1, matrix products, volume_terms(): jnp.einsum('anm,qms->qans', deriv_mats, coefficients, precision=exact_prec)  10.5 us
  transfers between devices with their start and end apart: 4, of which 4 were waited for; matrix products, arithmetic and copies ran while one was open for 13% of the time, Pallas kernels for 0%

profile of v1, /device:TPU:1, one launch (start us, length us, event | category | flops | bytes accessed | tf_op | source)
XLA Modules:
  0.0 284.6 jit_solution(8667546582597997317)
XLA Ops:
  0.7 4.3 %scatter_custom_fusion = s32[2048]{0:T(1024)S(1)} fusion(s32[1024]{0:T(1024)S(1)} %compare_select_fusion.3, s32[1024]{0:T(1024)S(1)} %iota.14, s32[]{:T(128)} %constant.33.clone.1), kind=kCustom, calls=%fused_computation.89 | custom fusion | bytes 8196 | tf_op jit(solution)/shard_map/scatter | solution.py:105
  10.5 6.6 %gather_fusion = f32[2048,235]{1,0:T(8,128)S(1)} fusion(f32[235,1025]{0,1:T(8,128)S(1)} %select_maximum_fusion, s32[2048]{0:T(1024)S(1)} %fusion.12), kind=kCustom, calls=%fused_computation | custom fusion | bytes 3858432 | tf_op jit(solution)/shard_map/jit(_take)/gather | solution.py:108
  22.4 3.2 %pad_maximum_fusion.1 = f32[4,235,1,512]{3,2,1,0:T(1,128)} fusion(f32[1,235,1,512]{3,2,1,0:T(1,128)S(1)} %get-tuple-element.27, f32[1,235,1,512]{3,2,1,0:T(1,128)S(1)} %get-tuple-element.28, f32[1,235,1,512]{3,2,1,0:T(1,128)S(1)} %get-tuple-element.29, f32[1,235,1,512]{3,2,1,0:T(1,128)S(1)} %get-tuple-element.26), kind=kLoop, calls=%fused_computation.11 | loop fusion | flops 1443840 | bytes 3850240 | tf_op jit(solution)/shard_map/stack | solution.py:111
  25.6 4.7 %all-to-all-start = ((f32[4,235,1,512]{3,2,1,0:T(1,128)}), f32[4,235,1,512]{3,2,1,0:T(1,128)S(1)}, u32[]{:S(2)}, u32[]{:S(2)}) async-start(f32[4,235,1,512]{3,2,1,0:T(1,128)} %pad_maximum_fusion.1), calls=%async_computation | async-start | bytes 3850240 | tf_op jit(solution)/shard_map/all_to_all | solution.py:110
  32.8 20.0 %all-to-all-done = f32[4,235,1,512]{3,2,1,0:T(1,128)S(1)} async-done(((f32[4,235,1,512]{3,2,1,0:T(1,128)}), f32[4,235,1,512]{3,2,1,0:T(1,128)S(1)}, u32[]{:S(2)}, u32[]{:S(2)}) %all-to-all-start) | async-done | bytes 1925152 | tf_op jit(solution)/shard_map/all_to_all | solution.py:110
  59.9 4.7 %convolution_bitcast_fusion.1 = f32[6,60,2048]{2,1,0:T(8,128)S(1)} fusion(f32[6,35,2048]{2,1,0:T(8,128)} %reshape.2023, f32[1,60,35]{1,0,2:T(1,128)S(1)} %broadcast_multiply_fusion), kind=kOutput, calls=%fused_computation.7 | convolution fusion | flops 309657600 | bytes 4677840 | tf_op jit(solution)/shard_map/pm,qms->qps/dot_general | solution.py:123
  64.6 3.0 %reshape.2024 = f32[90,8192]{1,0:T(8,128)} reshape(f32[6,60,2048]{2,1,0:T(8,128)S(1)} %convolution_bitcast_fusion.1) | data formatting | bytes 5898240 | tf_op jit(solution)/shard_map/reshape | solution.py:123
  67.6 5.2 %copy.142 = f32[90,8192]{0,1:T(8,128)} copy(f32[90,8192]{1,0:T(8,128)} %reshape.2024) | data formatting | bytes 5898240 | tf_op jit(solution)/shard_map/reshape | solution.py:123
  72.8 3.8 %concatenate.15 = f32[8193,90]{1,0:T(8,128)} pad(f32[8192,90]{1,0:T(8,128)} %bitcast.203, f32[]{:T(128)} %constant.45.clone.1), padding=0_1x0_0 | pad | bytes 5898604 | tf_op jit(solution)/shard_map/concatenate | solution.py:126
  76.6 33.3 %gather_fusion.1 = f32[9216,90]{1,0:T(8,128)} fusion(f32[8193,90]{1,0:T(8,128)} %concatenate.15, s32[9216]{0:T(1024)S(1)} %fusion.4), kind=kCustom, calls=%fused_computation.1 | custom fusion | bytes 6672384 | tf_op jit(solution)/shard_map/jit(_take)/gather | solution.py:129
  109.9 3.9 %copy.143 = f32[3,4,768,90]{2,3,0,1:T(8,128)S(1)} copy(f32[3,4,768,90]{3,2,1,0:T(8,128)} %bitcast.201) | data formatting | bytes 6635520 | tf_op jit(solution)/shard_map/jit(_take)/gather | solution.py:129
  116.0 4.3 %all-to-all-start.1 = ((f32[3,4,768,90]{2,3,0,1:T(8,128)}), f32[3,4,768,90]{2,3,0,1:T(8,128)S(1)}, u32[]{:S(2)}, u32[]{:S(2)}) async-start(f32[3,4,768,90]{2,3,0,1:T(8,128)} %broadcast_select_fusion), calls=%async_computation.1 | async-start | bytes 7077888 | tf_op jit(solution)/shard_map/all_to_all | solution.py:83
  120.3 10.5 %convolution_bitcast_fusion = f32[6,3,35,2048]{3,2,1,0:T(8,128)} fusion(f32[6,35,2048,1]{2,1,0,3:T(8,128)} %reshape.2063, f32[3,35,35]{2,1,0:T(8,128)} %copy.140), kind=kOutput, calls=%fused_computation.5 | convolution fusion | flops 541900800 | bytes 6895980 | tf_op jit(solution)/shard_map/anm,qms->qans/dot_general | solution.py:31
  144.6 15.5 %all-to-all-done.1 = f32[3,4,768,90]{2,3,0,1:T(8,128)S(1)} async-done(((f32[3,4,768,90]{2,3,0,1:T(8,128)}), f32[3,4,768,90]{2,3,0,1:T(8,128)S(1)}, u32[]{:S(2)}, u32[]{:S(2)}) %all-to-all-start.1) | async-done | bytes 3317792 | tf_op jit(solution)/shard_map/all_to_all | solution.py:83
  176.7 7.9 %collective-permute-done.1 = f32[4,768,90]{1,0,2:T(4,128)S(1)} collective-permute-done((f32[4,768,90]{1,0,2:T(4,128)S(1)}, f32[4,768,90]{1,0,2:T(4,128)S(1)}, u32[]{:S(2)}, u32[]{:S(2)}) %collective-permute-start.1) | collective-permute-done | bytes 1105952 | tf_op jit(solution)/shard_map/ppermute | solution.py:14
  184.8 6.6 %collective-permute-done = f32[4,768,90]{1,0,2:T(4,128)} collective-permute-done((f32[4,768,90]{1,0,2:T(4,128)}, f32[4,768,90]{1,0,2:T(4,128)}, u32[]{:S(2)}, u32[]{:S(2)}) %collective-permute-start) | collective-permute-done | bytes 1105952 | tf_op jit(solution)/shard_map/ppermute | solution.py:14
  193.2 3.6 %copy.148 = f32[3,4,768,90]{3,2,1,0:T(8,128)} copy(f32[3,4,768,90]{2,3,0,1:T(8,128)S(1)} %pad_maximum_fusion) | data formatting | bytes 6635520 | tf_op jit(solution)/shard_map/stack | solution.py:89
  196.8 4.0 %concatenate.16 = f32[9217,90]{1,0:T(8,128)} pad(f32[9216,90]{1,0:T(8,128)} %bitcast.202, f32[]{:T(128)} %constant.45.clone.1), padding=0_1x0_0 | pad | bytes 6635884 | tf_op jit(solution)/shard_map/concatenate | solution.py:131
  200.7 30.0 %gather_fusion.2 = f32[8192,90]{1,0:T(8,128)} fusion(f32[9217,90]{1,0:T(8,128)} %concatenate.16, s32[8192]{0:T(1024)S(1)} %copy-done.25), kind=kCustom, calls=%fused_computation.2 | custom fusion | bytes 5931008 | tf_op jit(solution)/shard_map/jit(_take)/gather | solution.py:134
  230.8 6.2 %select_bitcast_fusion = f32[90,8192]{0,1:T(8,128)S(1)} fusion(f32[8192,90]{1,0:T(8,128)} %gather_fusion.2, pred[8192]{0:T(1024)(128)(4,1)S(1)} %copy-done.27), kind=kLoop, calls=%fused_computation.4 | loop fusion | flops 737280 | bytes 5906432 | tf_op jit(solution)/shard_map/jit(_take)/select_n | solution.py:134
  237.0 11.1 %fusion.15 = (f32[15,8192]{0,1:T(8,128)}, f32[15,8192]{0,1:T(8,128)}, f32[15,8192]{0,1:T(8,128)}, f32[15,8192]{0,1:T(8,128)}, f32[15,8192]{0,1:T(8,128)}, /*index=5*/f32[15,8192]{0,1:T(8,128)}) fusion(f32[90,8192]{0,1:T(8,128)S(1)} %select_bitcast_fusion), kind=kLoop, calls=%fused_computation.92 | loop fusion | bytes 5898240 | tf_op jit(solution)/shard_map/slice | solution.py:57
  267.1 3.9 %copy.154 = f32[15,8192]{1,0:T(8,128)} copy(f32[15,8192]{0,1:T(8,128)} %get-tuple-element.13) | data formatting | bytes 983040 | tf_op jit(solution)/shard_map/slice | solution.py:57
  273.1 3.2 %multiply_dynamic-update-slice_fusion.5 = (f32[6,60,2048]{2,1,0:T(8,128)S(1)}, f32[1,60,2048]{2,1,0:T(8,128)S(1)}, f32[1,60,2048]{2,1,0:T(8,128)S(1)}, f32[1,60,...) fusion(f32[1,60,2048]{2,1,0:T(8,128)} %mul.929, f32[1,60,2048]{2,1,0:T(8,128)} %mul.943, ...), kind=kLoop, calls=%fused_computation.35 | loop fusion | flops 2088959 | bytes 10027008
  278.7 4.2 %fusion = f32[6,35,2048]{2,1,0:T(8,128)S(1)} fusion(f32[6,35,2048]{2,1,0:T(8,128)} %negate_dynamic-update-slice_fusion, f32[6,60,2048]{2,1,0:T(8,128)S(1)} %multiply_dynamic-update-slice_fusion, f32[1,35,60]{2,0,1:T(1,128)S(1)} %copy-done.28, f32[35]{0:T(128)S(1)} %copy-done.33), kind=kOutput, calls=%fused_computation.9 | convolution fusion | flops 310089792 | bytes 6398300 | tf_op jit(solution)/shard_map/mp,qps->qms/dot_general | solution.py:78
  (146 shorter events, 80.1 us)
Async XLA Ops:
  0.0 7.7 %copy-start.26 = (f32[12,1024]{1,0:T(8,128)S(1)}, f32[12,1024]{1,0:T(8,128)}, u32[]{:S(2)}) copy-start(f32[12,1024]{1,0:T(8,128)} %param.13) | copy-start | bytes 147460
  0.0 7.9 %copy-start.31 = (f32[4,1024]{1,0:T(4,128)S(1)}, f32[4,1024]{1,0:T(4,128)}, u32[]{:S(2)}) copy-start(f32[4,1024]{1,0:T(4,128)} %param.14) | copy-start | bytes 49156
  25.6 4.7 %copy-start.23 = (s32[9216]{0:T(1024)S(1)}, s32[9216]{0:T(1024)}, u32[]{:S(2)}) copy-start(s32[9216]{0:T(1024)} %param.17) | copy-start | bytes 110596
  25.6 4.9 %copy-start.29 = (f32[1,105,35]{1,0,2:T(1,128)S(1)}, f32[1,105,35]{1,0,2:T(1,128)}, u32[]{:S(2)}) copy-start(f32[1,105,35]{1,0,2:T(1,128)} %param.19) | copy-start | bytes 44104
  25.6 5.9 %copy-start.30 = (f32[1,60,35]{1,0,2:T(1,128)S(1)}, f32[1,60,35]{1,0,2:T(1,128)}, u32[]{:S(2)}) copy-start(f32[1,60,35]{1,0,2:T(1,128)} %param.20) | copy-start | bytes 25204
  25.6 6.0 %copy-start.24 = (s32[8192]{0:T(1024)S(1)}, s32[8192]{0:T(1024)}, u32[]{:S(2)}) copy-start(s32[8192]{0:T(1024)} %param.18) | copy-start | bytes 98308
  25.6 27.2 %all-to-all-start = ((f32[4,235,1,512]{3,2,1,0:T(1,128)}), f32[4,235,1,512]{3,2,1,0:T(1,128)S(1)}, u32[]{:S(2)}, u32[]{:S(2)}) async-start(f32[4,235,1,512]{3,2,1,0:T(1,128)} %pad_maximum_fusion.1), calls=%async_computation | async-start | bytes 3850240 | tf_op jit(solution)/shard_map/all_to_all | solution.py:110
  30.4 22.9 %copy-start.32 = (f32[35]{0:T(128)}, f32[35]{0:T(128)S(1)}, u32[]{:S(2)}) copy-start(f32[35]{0:T(128)S(1)} %compare_convert_fusion) | copy-start | bytes 424
  116.0 44.1 %all-to-all-start.1 = ((f32[3,4,768,90]{2,3,0,1:T(8,128)}), f32[3,4,768,90]{2,3,0,1:T(8,128)S(1)}, u32[]{:S(2)}, u32[]{:S(2)}) async-start(f32[3,4,768,90]{2,3,0,1:T(8,128)} %broadcast_select_fusion), calls=%async_computation.1 | async-start | bytes 7077888 | tf_op jit(solution)/shard_map/all_to_all | solution.py:83
  134.9 4.8 %copy-start.9 = (f32[1,1,2048]{2,1,0:T(1,128)}, f32[1,1,2048]{2,1,0:T(1,128)S(1)}, u32[]{:S(2)}) copy-start(f32[1,1,2048]{2,1,0:T(1,128)S(1)} %get-tuple-element.32) | copy-start | bytes 24580
  134.9 7.2 %copy-start.11 = (f32[1,1,2048]{2,1,0:T(1,128)}, f32[1,1,2048]{2,1,0:T(1,128)S(1)}, u32[]{:S(2)}) copy-start(f32[1,1,2048]{2,1,0:T(1,128)S(1)} %get-tuple-element.36) | copy-start | bytes 24580
  134.9 7.2 %copy-start.13 = (f32[1,1,2048]{2,1,0:T(1,128)}, f32[1,1,2048]{2,1,0:T(1,128)S(1)}, u32[]{:S(2)}) copy-start(f32[1,1,2048]{2,1,0:T(1,128)S(1)} %get-tuple-element.37) | copy-start | bytes 24580
  134.9 7.2 %copy-start.15 = (f32[1,1,2048]{2,1,0:T(1,128)}, f32[1,1,2048]{2,1,0:T(1,128)S(1)}, u32[]{:S(2)}) copy-start(f32[1,1,2048]{2,1,0:T(1,128)S(1)} %get-tuple-element.38) | copy-start | bytes 24580
  135.0 7.2 %copy-start.17 = (f32[1,1,2048]{2,1,0:T(1,128)}, f32[1,1,2048]{2,1,0:T(1,128)S(1)}, u32[]{:S(2)}) copy-start(f32[1,1,2048]{2,1,0:T(1,128)S(1)} %get-tuple-element.33) | copy-start | bytes 24580
  135.0 7.2 %copy-start.19 = (f32[1,1,2048]{2,1,0:T(1,128)}, f32[1,1,2048]{2,1,0:T(1,128)S(1)}, u32[]{:S(2)}) copy-start(f32[1,1,2048]{2,1,0:T(1,128)S(1)} %get-tuple-element.34) | copy-start | bytes 24580
  135.0 7.2 %copy-start.21 = (f32[1,1,2048]{2,1,0:T(1,128)}, f32[1,1,2048]{2,1,0:T(1,128)S(1)}, u32[]{:S(2)}) copy-start(f32[1,1,2048]{2,1,0:T(1,128)S(1)} %get-tuple-element.35) | copy-start | bytes 24580
  162.0 22.5 %collective-permute-start.1 = (f32[4,768,90]{1,0,2:T(4,128)S(1)}, f32[4,768,90]{1,0,2:T(4,128)S(1)}, u32[]{:S(2)}, u32[]{:S(2)}) collective-permute-start(f32[4,768,90]{1,0,2:T(4,128)S(1)} %copy.146), channel_id=1, source_target_pairs={{0,1},{1,2},{2,3},{3,4},{4,5},{5,6},{6,7},{7,0},{8,9},{9,10},{10,1... | collective-permute-start | bytes 3317768 | tf_op jit(solution)/shard_map/ppermute | solution.py:14
  166.5 24.9 %collective-permute-start = (f32[4,768,90]{1,0,2:T(4,128)}, f32[4,768,90]{1,0,2:T(4,128)}, u32[]{:S(2)}, u32[]{:S(2)}) collective-permute-start(f32[4,768,90]{1,0,2:T(4,128)} %copy.144), channel_id=1, source_target_pairs={{0,7},{1,0},{2,1},{3,2},{4,3},{5,4},{6,5},{7,6},{8,15},{9,8},{10,9... | collective-permute-start | bytes 3317768 | tf_op jit(solution)/shard_map/ppermute | solution.py:14
  170.8 3.5 %copy-start.14 = (f32[1,1,2048]{2,1,0:T(1,128)S(1)}, f32[1,1,2048]{2,1,0:T(1,128)}, u32[]{:S(2)}) copy-start(f32[1,1,2048]{2,1,0:T(1,128)} %copy-done.13) | copy-start | bytes 24580
  170.8 3.5 %copy-start.16 = (f32[1,1,2048]{2,1,0:T(1,128)S(1)}, f32[1,1,2048]{2,1,0:T(1,128)}, u32[]{:S(2)}) copy-start(f32[1,1,2048]{2,1,0:T(1,128)} %copy-done.15) | copy-start | bytes 24580
  176.7 16.2 %copy-start.7 = (f32[1,4,768,90]{2,3,0,1:T(8,128)S(1)}, f32[1,4,768,90]{2,3,0,1:T(8,128)}, u32[]{:S(2)}) copy-start(f32[1,4,768,90]{2,3,0,1:T(8,128)} %get-tuple-element.21) | copy-start | bytes 3317764
  196.8 4.0 %copy-start.25 = (s32[8192]{0:T(1024)S(1)}, s32[8192]{0:T(1024)}, u32[]{:S(2)}) copy-start(s32[8192]{0:T(1024)} %fusion.5) | copy-start | bytes 98308
  200.7 30.0 %copy-start.27 = (pred[8192]{0:T(1024)(128)(4,1)S(1)}, pred[8192]{0:T(1024)(128)(4,1)}, u32[]{:S(2)}) copy-start(pred[8192]{0:T(1024)(128)(4,1)} %compare_and_fusion.1) | copy-start | bytes 24580
  267.1 5.9 %copy-start.1 = (f32[6,60,2048]{2,1,0:T(8,128)S(1)}, f32[6,60,2048]{2,1,0:T(8,128)}, u32[]{:S(2)}) copy-start(f32[6,60,2048]{2,1,0:T(8,128)} %copy-done) | copy-start | bytes 8847364
  (14 other events, 38.2 us)
